TPU v7x, 128 devices: a whole 4x4x4 slice. The times are simulated.
128 devices in a mesh: grid: 32 (over x, z, core), orb: 4 (over y).
Axes of the slice: x: 4, y: 4, z: 4, core: 2. Of those that a mesh axis runs over, the one named last changes fastest.
Arguments:
- orbitals: bfloat16 [1800, 262144], P('orb', 'grid'), may hold values from -0.5 to 1.5
- pivots: int32 [3, 96], replicated, may hold values from 0 to 262143, as said below
Outputs:
- cholesky_factor: float32 [262144, 288], P(('grid', 'orb'))
- residual_diagonal: float32 [262144], P(('grid', 'orb'))
- diagonal_peaks: float32 [3], replicated
Inputs may be any that keep to these rules, and one draw needn't show every extreme that they name: `pivots`: all 3 x 96 pivot indices are distinct grid points.
All inputs are finite; a program needn't handle non-finite values.
Results may differ from a plain program's by a relative error of at most 0.0003.
Values may be sent and summed in bfloat16 or wider, within the bound.
No kernel may reach another device: no remote copies, remote signals or barrier semaphores. Data moves between devices by JAX's collectives and lax.ppermute only.
A program may use at most 64 MiB of HBM per device.

v0:
```python
import jax
import jax.numpy as jnp
from jax import lax
from jax.sharding import Mesh
from jax.sharding import PartitionSpec as P

ORB = 1800
GRID = ("grid_0", "grid_1", "grid_2")
GRID_ORB = ("grid_0", "grid_1", "grid_2", "orb")


def from_everyone(x, axis):
    copies = jnp.broadcast_to(x, (lax.axis_size(axis), *x.shape))
    return lax.all_to_all(copies, axis, split_axis=0, concat_axis=0, tiled=True)


def laid_out(pieces, dim):
    pieces = jnp.moveaxis(pieces, 0, dim)
    lengths = pieces.shape
    return pieces.reshape(*lengths[:dim], lengths[dim] * lengths[dim + 1], *lengths[dim + 2 :])


def gather_directly(x, axis, dim):
    pieces = from_everyone(x, axis)
    return laid_out(pieces, dim)


def one_axis_at_a_time(x, axes):
    for axis in axes:
        x = lax.pmax(x, axis)
    return x


def pick_columns(values, index, base, count):
    local = index - base
    inside = (local >= 0) & (local < count)
    taken = jnp.take(values, jnp.clip(local, 0, count - 1), axis=1)
    return jnp.where(inside[None, :], taken, jnp.zeros_like(taken))


def contract_first(left, right):
    return lax.dot_general(
        left, right, (((0,), (0,)), ((), ())), preferred_element_type=jnp.float32
    )


def on_device(orbitals, pivots):
    rows = orbitals.shape[1]
    groups = lax.axis_size("orb")
    share = rows // groups
    sections = pivots.shape[0]
    count = pivots.shape[1]
    total_rank = sections * count
    grid_base = lax.axis_index(GRID) * rows
    squares = lax.psum_scatter(
        jnp.sum(jnp.square(orbitals.astype(jnp.float32)), axis=0),
        "orb",
        scatter_dimension=0,
        tiled=True,
    )
    diagonal = jnp.square(squares / ORB)
    factor = jnp.zeros((share, total_rank), jnp.float32)
    flat = pivots.reshape(total_rank)
    local_pivots = lax.psum(
        pick_columns(orbitals, flat, grid_base, rows).astype(jnp.float32).astype(jnp.bfloat16), GRID
    )
    whole = gather_directly(local_pivots, "orb", 0)
    pivot_pairs = contract_first(whole, whole)
    pivot_factor = jnp.zeros((total_rank, total_rank), jnp.float32)
    peaks = []
    for section in range(sections):
        lead = section * count
        sampled_here = lax.slice_in_dim(local_pivots, lead, lead + count, axis=1)
        known = lax.slice_in_dim(pivot_factor, lead, lead + count, axis=0)
        pair = lax.slice_in_dim(
            lax.slice_in_dim(pivot_pairs, lead, lead + count, axis=0), lead, lead + count, axis=1
        )

        def product(start, length, picked=sampled_here):
            return contract_first(orbitals, picked)

        inner = lax.psum_scatter(
            product(jnp.int32(0), share * lax.axis_size("orb")),
            "orb",
            scatter_dimension=0,
            tiled=True,
        )
        block = jnp.square(pair / ORB) - jnp.dot(known, known.T, precision=lax.Precision.HIGHEST)
        columns = jnp.square(inner / ORB) - jnp.dot(
            factor, known.T, precision=lax.Precision.HIGHEST
        )
        lower = jnp.linalg.cholesky(block)
        fresh = jax.scipy.linalg.solve_triangular(lower, columns.T, lower=True).T
        factor = factor.at[:, lead : lead + count].set(fresh)
        pivot_columns = jnp.square(
            lax.slice_in_dim(pivot_pairs, lead, lead + count, axis=1) / ORB
        ) - jnp.dot(pivot_factor, known.T, precision=lax.Precision.HIGHEST)
        pivot_fresh = jax.scipy.linalg.solve_triangular(lower, pivot_columns.T, lower=True).T
        pivot_factor = pivot_factor.at[:, lead : lead + count].set(pivot_fresh)
        diagonal = diagonal - jnp.sum(fresh * fresh, axis=1)
        peaks.append(one_axis_at_a_time(jnp.max(diagonal), GRID_ORB))
    peak_values = jnp.stack(peaks)
    return (factor, diagonal, peak_values)


def solution(mesh):
    split = Mesh(
        mesh.devices.reshape(4, 4, 2, mesh.shape["orb"]), ("grid_0", "grid_1", "grid_2", "orb")
    )
    placed = (P("orb", GRID), P())
    return jax.shard_map(
        on_device,
        mesh=split,
        in_specs=placed,
        out_specs=(P(GRID_ORB, None), P(GRID_ORB), P()),
        check_vma=False,
    )
```

profile of v0, /device:TPU:0, one launch (start us, length us, event | category | flops | bytes accessed | tf_op | source)
XLA Modules:
  0.0 320.0 jit_solution(15605662126289330419)
XLA Ops:
  8.8 11.6 %copy.15 = bf16[450,8192]{0,1:T(8,128)(2,1)} copy(bf16[450,8192]{1,0:T(8,128)(2,1)} %param.17) | data formatting | bytes 14745600 | tf_op args[0]
  20.5 6.5 %gather_fusion = bf16[288,450]{1,0:T(8,128)(2,1)S(1)} fusion(bf16[450,8192]{0,1:T(8,128)(2,1)} %copy.15, s32[1024]{0:T(1024)S(1)} %pad_clamp_fusion), kind=kCustom, calls=%fused_computation | custom fusion | bytes 519552 | tf_op jit(solution)/shard_map/jit(_take)/gather | solution.py:37
  27.0 0.9 select_bitcast_fusion.1
  27.9 104.7 %all-reduce.9.cloned.1.call-done = bf16[450,288]{0,1:T(8,128)(2,1)} async-done(((bf16[450,288]{0,1:T(8,128)(2,1)}), bf16[450,288]{0,1:T(8,128)(2,1)}) %all-reduce.9.cloned.1.call-update) | async-done | bytes 259216 | tf_op jit(solution)/shard_map/psum | solution.py:64
  132.7 6.3 %convolution_bitcast_fusion.2 = f32[8192,96]{0,1:T(8,128)} fusion(bf16[450,8192]{1,0:T(8,128)(2,1)} %param.17, bf16[450,288]{0,1:T(8,128)(2,1)} %all-reduce.9.cloned.1.call-done), kind=kOutput, calls=%fused_computation.4 | convolution fusion | flops 707788800 | bytes 10715136 | tf_op jit(solution)/shard_map/dot_general | solution.py:42
  139.1 0.9 copy-done.2
  140.0 6.3 %convolution_bitcast_fusion.1 = f32[8192,96]{0,1:T(8,128)} fusion(bf16[450,8192]{1,0:T(8,128)(2,1)} %param.17, bf16[450,288]{0,1:T(8,128)(2,1)S(1)} %copy-done.2), kind=kOutput, calls=%fused_computation.3 | convolution fusion | flops 707788800 | bytes 10616832 | tf_op jit(solution)/shard_map/dot_general | solution.py:42
  146.3 6.6 %convolution_bitcast_fusion = f32[8192,96]{0,1:T(8,128)} fusion(bf16[450,8192]{1,0:T(8,128)(2,1)} %param.17, bf16[450,288]{0,1:T(8,128)(2,1)S(1)} %copy-done.2), kind=kOutput, calls=%fused_computation.2 | convolution fusion | flops 707788800 | bytes 10616832 | tf_op jit(solution)/shard_map/dot_general | solution.py:42
  152.9 1.1 broadcast_in_dim.32
  154.1 4.3 %all-to-all-start = ((bf16[4,450,288]{1,2,0:T(8,128)(2,1)}), bf16[4,450,288]{1,2,0:T(8,128)(2,1)S(1)}, u32[]{:S(2)}, u32[]{:S(2)}) async-start(bf16[4,450,288]{1,2,0:T(8,128)(2,1)} %broadcast_in_dim.32), calls=%async_computation | async-start | bytes 2359296 | tf_op jit(solution)/shard_map/all_to_all | solution.py:14
  161.0 4.8 %multiply_reduce_fusion = f32[8192]{0:T(1024)S(1)} fusion(bf16[450,8192]{1,0:T(8,128)(2,1)} %param.17), kind=kLoop, calls=%fused_computation.1 | loop fusion | flops 11051008 | bytes 7405568 | tf_op jit(solution)/shard_map/reduce_sum | solution.py:56
  165.8 31.0 %all-reduce.2 = f32[8192]{0:T(1024)S(1)} all-reduce(f32[8192]{0:T(1024)S(1)} %multiply_reduce_fusion), channel_id=5, replica_groups=mesh['grid_0'=4,'grid_1'=4,'grid_2'=2,'orb'=4] {'orb'}, use_global_device_ids=true, to_apply=%region_9.13.clone | all-reduce | flops 8192 | bytes 65536
  198.1 8.8 %cholesky.59 = f32[96,96]{1,0:T(8,128)S(1)} custom-call(f32[96,96]{1,0:T(8,128)S(1)} %fusion.36), custom_call_target="Cholesky" | custom-call | tf_op jit(solution)/shard_map/jit(cholesky)/cholesky | solution.py:92
  208.2 7.4 %custom-call.11 = f32[1,96,96]{1,2,0:T(8,128)S(1)} custom-call(f32[1,96,96]{2,1,0:T(8,128)S(1)} %fusion.25), custom_call_target="InvertDiagBlocksLowerTriangular" | custom-call | tf_op jit(solution)/shard_map/jit(_solve_triangular)/triangular_solve | solution.py:93
  215.7 1.0 fusion.5
  217.2 8.8 %cholesky.70 = f32[96,96]{1,0:T(8,128)S(1)} custom-call(f32[96,96]{1,0:T(8,128)S(1)} %fusion.33), custom_call_target="Cholesky" | custom-call | tf_op jit(solution)/shard_map/jit(cholesky)/cholesky | solution.py:92
  227.4 7.4 %custom-call.13 = f32[1,96,96]{1,2,0:T(8,128)S(1)} custom-call(f32[1,96,96]{2,1,0:T(8,128)S(1)} %fusion.26), custom_call_target="InvertDiagBlocksLowerTriangular" | custom-call | tf_op jit(solution)/shard_map/jit(_solve_triangular)/triangular_solve | solution.py:93
  235.4 1.0 fusion.4
  237.1 8.9 %cholesky.81 = f32[96,96]{1,0:T(8,128)S(1)} custom-call(f32[96,96]{1,0:T(8,128)S(1)} %fusion.29), custom_call_target="Cholesky" | custom-call | tf_op jit(solution)/shard_map/jit(cholesky)/cholesky | solution.py:92
  247.4 7.4 %custom-call.15 = f32[1,96,96]{1,2,0:T(8,128)S(1)} custom-call(f32[1,96,96]{2,1,0:T(8,128)S(1)} %fusion.27), custom_call_target="InvertDiagBlocksLowerTriangular" | custom-call | tf_op jit(solution)/shard_map/jit(_solve_triangular)/triangular_solve | solution.py:93
  254.8 2.7 multiply_reduce_fusion.3
  257.7 2.3 fusion.1
  260.1 1.5 bitcast_dynamic-update-slice_fusion
  261.6 8.3 %reduce-scatter.8.cloned.1.call-done = f32[2048,96]{0,1:T(8,128)} async-done(((f32[8192,96]{0,1:T(8,128)}), f32[2048,96]{0,1:T(8,128)}) %reduce-scatter.8.cloned.1.call-update) | async-done | bytes 786448 | tf_op jit(solution)/shard_map/reduce_scatter | solution.py:82
  270.0 3.3 %fusion = f32[96,2048]{1,0:T(8,128)S(1)} fusion(f32[2048,288]{0,1:T(8,128)S(1)} %get-tuple-element.90, f32[2048,96]{0,1:T(8,128)} %reduce-scatter.8.cloned.1.call-done, f32[288,288]{0,1:T(8,128)} %copy-done.1), kind=kOutput, calls=%fused_computation.7 | convolution fusion | flops 680067072 | bytes 4079616 | tf_op jit(solution)/shard_map/dot_general | solution.py:89
  273.3 0.9 multiply_reduce_fusion.1
  274.9 1.3 fusion.48
  276.2 11.1 %all-reduce.5 = (f32[]{:T(128)}, f32[]{:T(128)}, f32[]{:T(128)}) all-reduce(f32[]{:T(128)} %get-tuple-element.81, f32[]{:T(128)} %get-tuple-element.67, f32[]{:T(128)} %get-tuple-element.66), channel_id=1, replica_groups=mesh['grid_0'=4,'grid_1'=4,'grid_2'=2,'orb'=4] {'grid_0'}, use_global_device_ids=true, to_apply=%region_24.28 | all-reduce | flops 3 | bytes 24 | tf_op jit(solution)/shard_map/pmax | solution.py:30
  287.3 11.3 %all-reduce.4 = (f32[]{:T(128)}, f32[]{:T(128)}, f32[]{:T(128)}) all-reduce(f32[]{:T(128)} %get-tuple-element.74, f32[]{:T(128)} %get-tuple-element.75, f32[]{:T(128)} %get-tuple-element.76), channel_id=1, replica_groups=mesh['grid_0'=4,'grid_1'=4,'grid_2'=2,'orb'=4] {'grid_1'}, use_global_device_ids=true, to_apply=%region_25.29 | all-reduce | flops 3 | bytes 24 | tf_op jit(solution)/shard_map/pmax | solution.py:30
  298.6 3.2 all-reduce.6
  301.8 9.2 %all-reduce.3 = (f32[1]{0:T(128)}, f32[1]{0:T(128)}, f32[1]{0:T(128)}) all-reduce(f32[1]{0:T(128)} %bitcast.30, f32[1]{0:T(128)} %bitcast.29, f32[1]{0:T(128)} %bitcast.28), channel_id=1, replica_groups=mesh['grid_0'=4,'grid_1'=4,'grid_2'=2,'orb'=4] {'orb'}, use_global_device_ids=true, to_apply=%region_27.31 | all-reduce | flops 3 | bytes 24 | tf_op jit(solution)/shard_map/pmax | solution.py:30
  311.0 2.5 pad_maximum_fusion
  (57 shorter events, 12.1 us)
Async XLA Ops:
  7.2 125.5 %all-reduce.9.cloned.1.call-start = ((), (), s32[]{:S(2)}) async-start(), calls=%async_computation.4 | async-start | bytes 589824 | tf_op jit(solution)/shard_map/psum | solution.py:64
  27.9 226.9 %reduce-scatter.4.cloned.1.call-start = ((), (), s32[]{:S(2)}) async-start(), calls=%async_computation.5 | async-start | bytes 3932160 | tf_op jit(solution)/shard_map/reduce_scatter | solution.py:82
  139.0 1.0 copy-start.2
  139.0 118.7 %reduce-scatter.6.cloned.1.call-start = ((), (), s32[]{:S(2)}) async-start(), calls=%async_computation.6 | async-start | bytes 3932160 | tf_op jit(solution)/shard_map/reduce_scatter | solution.py:82
  146.3 123.7 %reduce-scatter.8.cloned.1.call-start = ((), (), s32[]{:S(2)}) async-start(), calls=%async_computation.7 | async-start | bytes 3932160 | tf_op jit(solution)/shard_map/reduce_scatter | solution.py:82
  152.9 5.5 %copy-start.3 = (u32[128]{0:T(128)S(1)}, u32[128]{0:T(128)}, u32[]{:S(2)}) copy-start(u32[128]{0:T(128)} %constant.233) | copy-start | bytes 1540
  154.1 42.7 %all-to-all-start = ((bf16[4,450,288]{1,2,0:T(8,128)(2,1)}), bf16[4,450,288]{1,2,0:T(8,128)(2,1)S(1)}, u32[]{:S(2)}, u32[]{:S(2)}) async-start(bf16[4,450,288]{1,2,0:T(8,128)(2,1)} %broadcast_in_dim.32), calls=%async_computation | async-start | bytes 2359296 | tf_op jit(solution)/shard_map/all_to_all | solution.py:14
  236.4 21.0 %copy-start.1 = (f32[288,288]{0,1:T(8,128)}, f32[288,288]{0,1:T(8,128)S(1)}, u32[]{:S(2)}) copy-start(f32[288,288]{0,1:T(8,128)S(1)} %fusion.4) | copy-start | bytes 995332
  274.1 39.3 %copy-start = (f32[2048,288]{0,1:T(8,128)}, f32[2048,288]{0,1:T(8,128)S(1)}, u32[]{:S(2)}) copy-start(f32[2048,288]{0,1:T(8,128)S(1)} %get-tuple-element.86) | copy-start | bytes 7077892
Sparse Core Ops, SparseCore 0:
  28.0 104.6 all-reduce.8
  139.1 49.4 reduce-scatter.3
  191.1 38.4 reduce-scatter.5
  231.8 38.0 reduce-scatter.7
where the time goes:
time: 321 us; the launch traced here: 320 us
  waiting for transfers between devices  113 us (35%)
  blocking collectives  65.8 us (20%)
  other arithmetic  65.6 us (20%)
  matrix products  34.5 us (11%)
  local copies, waits for them, and re-layouts  21.8 us (7%)
  between operations  14.8 us (5%)
  starting transfers between devices  4.49 us (1%)
    psum x1, waiting for transfers between devices, on_device(): lax.psum(pick_columns(orbitals, flat, grid_base, rows).astype(jnp.float32...  105 us
    pmax x4, blocking collectives, one_axis_at_a_time(): x = lax.pmax(x, axis)  34.8 us
    unnamed x1, blocking collectives  31 us
    another operation x9, other arithmetic, on_device(): lower = jnp.linalg.cholesky(block)  28.5 us
    another operation x6, other arithmetic, on_device(): fresh = jax.scipy.linalg.solve_triangular(lower, columns.T, lower=True).T  24 us
    dot_general x4, matrix products, contract_first(): lax.dot_general(left, right, (((0,), (0,)), ((), ())), preferred_element_...  20 us
    unnamed x13, local copies, waits for them, and re-layouts  13.3 us
    reduce_scatter x3, waiting for transfers between devices, on_device(): lax.psum_scatter(product(jnp.int32(0), share * lax.axis_size('orb')), 'or...  8.36 us
  transfers between devices with their start and end apart: 5, of which 2 were waited for; matrix products, arithmetic and copies ran while one was open for 27% of the time, Pallas kernels for 0%

commit v1 on v0

--- a/solution.py
+++ b/solution.py
@@ -3,6 +3,7 @@
 from jax import lax
 from jax.sharding import Mesh
 from jax.sharding import PartitionSpec as P
+from jax.lax import psum
 
 ORB = 1800
 GRID = ("grid_0", "grid_1", "grid_2")
@@ -61,9 +62,11 @@
     diagonal = jnp.square(squares / ORB)
     factor = jnp.zeros((share, total_rank), jnp.float32)
     flat = pivots.reshape(total_rank)
-    local_pivots = lax.psum(
-        pick_columns(orbitals, flat, grid_base, rows).astype(jnp.float32).astype(jnp.bfloat16), GRID
+    local_pivots = (
+        pick_columns(orbitals, flat, grid_base, rows).astype(jnp.float32).astype(jnp.bfloat16)
     )
+    for jj in (("grid_1", "grid_2"), "grid_0"):
+        local_pivots = psum(local_pivots, jj)
     whole = gather_directly(local_pivots, "orb", 0)
     pivot_pairs = contract_first(whole, whole)
     pivot_factor = jnp.zeros((total_rank, total_rank), jnp.float32)

time: 321 us -> 324 us (level)
    psum x1 -> x2, waiting for transfers between devices: 105 us -> 106 us  [on_device(): local_pivots = psum(local_pivots, jj)]
  transfers between devices with their start and end apart: 5 -> 6, of which waited for: 2 -> 3; matrix products, arithmetic and copies ran while one was open for 27% -> 26% of each run, Pallas kernels for 0% -> 0%
where the time goes in v1:
time: 324 us; the launch traced here: 323 us
  waiting for transfers between devices  116 us (36%)
  blocking collectives  66 us (20%)
  other arithmetic  65.6 us (20%)
  matrix products  34.8 us (11%)
  local copies, waits for them, and re-layouts  21.8 us (7%)
  between operations  14.8 us (5%)
  starting transfers between devices  4.48 us (1%)
    psum x2, waiting for transfers between devices, on_device(): local_pivots = psum(local_pivots, jj)  106 us
    pmax x4, blocking collectives, one_axis_at_a_time(): x = lax.pmax(x, axis)  34.9 us
    unnamed x1, blocking collectives  31.2 us
    another operation x9, other arithmetic, on_device(): lower = jnp.linalg.cholesky(block)  28.5 us
    another operation x6, other arithmetic, on_device(): fresh = jax.scipy.linalg.solve_triangular(lower, columns.T, lower=True).T  24 us
    dot_general x4, matrix products, contract_first(): lax.dot_general(left, right, (((0,), (0,)), ((), ())), preferred_element_...  20.4 us
    unnamed x13, local copies, waits for them, and re-layouts  13.3 us
    reduce_scatter x3, waiting for transfers between devices, on_device(): lax.psum_scatter(product(jnp.int32(0), share * lax.axis_size('orb')), 'or...  9.53 us
  transfers between devices with their start and end apart: 6, of which 3 were waited for; matrix products, arithmetic and copies ran while one was open for 26% of the time, Pallas kernels for 0%

profile of v1, /device:TPU:0, one launch (start us, length us, event | category | flops | bytes accessed | tf_op | source)
XLA Modules:
  0.0 323.3 jit_solution(10848617563473438924)
XLA Ops:
  8.8 11.6 %copy.15 = bf16[450,8192]{0,1:T(8,128)(2,1)} copy(bf16[450,8192]{1,0:T(8,128)(2,1)} %param.17) | data formatting | bytes 14745600 | tf_op args[0]
  20.5 6.5 %gather_fusion = bf16[288,450]{1,0:T(8,128)(2,1)S(1)} fusion(bf16[450,8192]{0,1:T(8,128)(2,1)} %copy.15, s32[1024]{0:T(1024)S(1)} %pad_clamp_fusion), kind=kCustom, calls=%fused_computation | custom fusion | bytes 519552 | tf_op jit(solution)/shard_map/jit(_take)/gather | solution.py:38
  27.9 63.4 %all-reduce.10.cloned.1.call-done = bf16[450,288]{0,1:T(8,128)(2,1)} async-done(((bf16[450,288]{0,1:T(8,128)(2,1)}), bf16[450,288]{0,1:T(8,128)(2,1)}) %all-reduce.10.cloned.1.call-update) | async-done | bytes 259216 | tf_op jit(solution)/shard_map/psum | solution.py:69
  91.4 42.9 %all-reduce.12.cloned.1.call-done = bf16[450,288]{0,1:T(8,128)(2,1)} async-done(((bf16[450,288]{0,1:T(8,128)(2,1)}), bf16[450,288]{0,1:T(8,128)(2,1)}) %all-reduce.12.cloned.1.call-update) | async-done | bytes 259216 | tf_op jit(solution)/shard_map/psum | solution.py:69
  134.3 6.3 %convolution_bitcast_fusion.2 = f32[8192,96]{0,1:T(8,128)} fusion(bf16[450,8192]{1,0:T(8,128)(2,1)} %param.17, bf16[450,288]{0,1:T(8,128)(2,1)} %all-reduce.12.cloned.1.call-done), kind=kOutput, calls=%fused_computation.4 | convolution fusion | flops 707788800 | bytes 10715136 | tf_op jit(solution)/shard_map/dot_general | solution.py:43
  140.7 0.9 copy-done.2
  141.6 6.3 %convolution_bitcast_fusion.1 = f32[8192,96]{0,1:T(8,128)} fusion(bf16[450,8192]{1,0:T(8,128)(2,1)} %param.17, bf16[450,288]{0,1:T(8,128)(2,1)S(1)} %copy-done.2), kind=kOutput, calls=%fused_computation.3 | convolution fusion | flops 707788800 | bytes 10616832 | tf_op jit(solution)/shard_map/dot_general | solution.py:43
  148.0 6.9 %convolution_bitcast_fusion = f32[8192,96]{0,1:T(8,128)} fusion(bf16[450,8192]{1,0:T(8,128)(2,1)} %param.17, bf16[450,288]{0,1:T(8,128)(2,1)S(1)} %copy-done.2), kind=kOutput, calls=%fused_computation.2 | convolution fusion | flops 707788800 | bytes 10616832 | tf_op jit(solution)/shard_map/dot_general | solution.py:43
  154.9 1.1 broadcast_in_dim.32
  156.0 4.3 %all-to-all-start = ((bf16[4,450,288]{1,2,0:T(8,128)(2,1)}), bf16[4,450,288]{1,2,0:T(8,128)(2,1)S(1)}, u32[]{:S(2)}, u32[]{:S(2)}) async-start(bf16[4,450,288]{1,2,0:T(8,128)(2,1)} %broadcast_in_dim.32), calls=%async_computation | async-start | bytes 2359296 | tf_op jit(solution)/shard_map/all_to_all | solution.py:15
  162.9 4.8 %multiply_reduce_fusion = f32[8192]{0:T(1024)S(1)} fusion(bf16[450,8192]{1,0:T(8,128)(2,1)} %param.17), kind=kLoop, calls=%fused_computation.1 | loop fusion | flops 11051008 | bytes 7405568 | tf_op jit(solution)/shard_map/reduce_sum | solution.py:57
  167.7 31.2 %all-reduce.2 = f32[8192]{0:T(1024)S(1)} all-reduce(f32[8192]{0:T(1024)S(1)} %multiply_reduce_fusion), channel_id=5, replica_groups=mesh['grid_0'=4,'grid_1'=4,'grid_2'=2,'orb'=4] {'orb'}, use_global_device_ids=true, to_apply=%region_10.14.clone | all-reduce | flops 8192 | bytes 65536
  200.2 8.8 %cholesky.59 = f32[96,96]{1,0:T(8,128)S(1)} custom-call(f32[96,96]{1,0:T(8,128)S(1)} %fusion.36), custom_call_target="Cholesky" | custom-call | tf_op jit(solution)/shard_map/jit(cholesky)/cholesky | solution.py:95
  210.4 7.4 %custom-call.11 = f32[1,96,96]{1,2,0:T(8,128)S(1)} custom-call(f32[1,96,96]{2,1,0:T(8,128)S(1)} %fusion.25), custom_call_target="InvertDiagBlocksLowerTriangular" | custom-call | tf_op jit(solution)/shard_map/jit(_solve_triangular)/triangular_solve | solution.py:96
  217.8 1.0 fusion.5
  219.3 8.8 %cholesky.70 = f32[96,96]{1,0:T(8,128)S(1)} custom-call(f32[96,96]{1,0:T(8,128)S(1)} %fusion.33), custom_call_target="Cholesky" | custom-call | tf_op jit(solution)/shard_map/jit(cholesky)/cholesky | solution.py:95
  229.5 7.4 %custom-call.13 = f32[1,96,96]{1,2,0:T(8,128)S(1)} custom-call(f32[1,96,96]{2,1,0:T(8,128)S(1)} %fusion.26), custom_call_target="InvertDiagBlocksLowerTriangular" | custom-call | tf_op jit(solution)/shard_map/jit(_solve_triangular)/triangular_solve | solution.py:96
  237.5 1.0 fusion.4
  239.2 8.9 %cholesky.81 = f32[96,96]{1,0:T(8,128)S(1)} custom-call(f32[96,96]{1,0:T(8,128)S(1)} %fusion.29), custom_call_target="Cholesky" | custom-call | tf_op jit(solution)/shard_map/jit(cholesky)/cholesky | solution.py:95
  249.5 7.4 %custom-call.15 = f32[1,96,96]{1,2,0:T(8,128)S(1)} custom-call(f32[1,96,96]{2,1,0:T(8,128)S(1)} %fusion.27), custom_call_target="InvertDiagBlocksLowerTriangular" | custom-call | tf_op jit(solution)/shard_map/jit(_solve_triangular)/triangular_solve | solution.py:96
  256.9 2.6 multiply_reduce_fusion.3
  259.8 2.3 fusion.1
  262.2 1.5 bitcast_dynamic-update-slice_fusion
  263.7 9.5 %reduce-scatter.8.cloned.1.call-done = f32[2048,96]{0,1:T(8,128)} async-done(((f32[8192,96]{0,1:T(8,128)}), f32[2048,96]{0,1:T(8,128)}) %reduce-scatter.8.cloned.1.call-update) | async-done | bytes 786448 | tf_op jit(solution)/shard_map/reduce_scatter | solution.py:85
  273.2 3.3 %fusion = f32[96,2048]{1,0:T(8,128)S(1)} fusion(f32[2048,288]{0,1:T(8,128)S(1)} %get-tuple-element.90, f32[2048,96]{0,1:T(8,128)} %reduce-scatter.8.cloned.1.call-done, f32[288,288]{0,1:T(8,128)} %copy-done.1), kind=kOutput, calls=%fused_computation.7 | convolution fusion | flops 680067072 | bytes 4079616 | tf_op jit(solution)/shard_map/dot_general | solution.py:92
  276.5 0.9 multiply_reduce_fusion.1
  278.2 1.3 fusion.48
  279.5 11.1 %all-reduce.5 = (f32[]{:T(128)}, f32[]{:T(128)}, f32[]{:T(128)}) all-reduce(f32[]{:T(128)} %get-tuple-element.81, f32[]{:T(128)} %get-tuple-element.67, f32[]{:T(128)} %get-tuple-element.66), channel_id=1, replica_groups=mesh['grid_0'=4,'grid_1'=4,'grid_2'=2,'orb'=4] {'grid_0'}, use_global_device_ids=true, to_apply=%region_25.29 | all-reduce | flops 3 | bytes 24 | tf_op jit(solution)/shard_map/pmax | solution.py:31
  290.5 11.4 %all-reduce.4 = (f32[]{:T(128)}, f32[]{:T(128)}, f32[]{:T(128)}) all-reduce(f32[]{:T(128)} %get-tuple-element.74, f32[]{:T(128)} %get-tuple-element.75, f32[]{:T(128)} %get-tuple-element.76), channel_id=1, replica_groups=mesh['grid_0'=4,'grid_1'=4,'grid_2'=2,'orb'=4] {'grid_1'}, use_global_device_ids=true, to_apply=%region_26.30 | all-reduce | flops 3 | bytes 24 | tf_op jit(solution)/shard_map/pmax | solution.py:31
  301.9 3.2 all-reduce.6
  305.0 9.3 %all-reduce.3 = (f32[1]{0:T(128)}, f32[1]{0:T(128)}, f32[1]{0:T(128)}) all-reduce(f32[1]{0:T(128)} %bitcast.30, f32[1]{0:T(128)} %bitcast.29, f32[1]{0:T(128)} %bitcast.28), channel_id=1, replica_groups=mesh['grid_0'=4,'grid_1'=4,'grid_2'=2,'orb'=4] {'orb'}, use_global_device_ids=true, to_apply=%region_28.32 | all-reduce | flops 3 | bytes 24 | tf_op jit(solution)/shard_map/pmax | solution.py:31
  314.3 2.5 pad_maximum_fusion
  (60 shorter events, 13.1 us)
Async XLA Ops:
  7.2 84.1 %all-reduce.10.cloned.1.call-start = ((), (), s32[]{:S(2)}) async-start(), calls=%async_computation.4 | async-start | bytes 589824 | tf_op jit(solution)/shard_map/psum | solution.py:69
  27.9 106.4 %all-reduce.12.cloned.1.call-start = ((), (), s32[]{:S(2)}) async-start(), calls=%async_computation.5 | async-start | bytes 589824 | tf_op jit(solution)/shard_map/psum | solution.py:69
  91.3 165.6 %reduce-scatter.4.cloned.1.call-start = ((), (), s32[]{:S(2)}) async-start(), calls=%async_computation.6 | async-start | bytes 3932160 | tf_op jit(solution)/shard_map/reduce_scatter | solution.py:85
  140.6 1.0 copy-start.2
  140.6 119.2 %reduce-scatter.6.cloned.1.call-start = ((), (), s32[]{:S(2)}) async-start(), calls=%async_computation.7 | async-start | bytes 3932160 | tf_op jit(solution)/shard_map/reduce_scatter | solution.py:85
  147.9 125.3 %reduce-scatter.8.cloned.1.call-start = ((), (), s32[]{:S(2)}) async-start(), calls=%async_computation.8 | async-start | bytes 3932160 | tf_op jit(solution)/shard_map/reduce_scatter | solution.py:85
  154.9 5.4 %copy-start.3 = (u32[128]{0:T(128)S(1)}, u32[128]{0:T(128)}, u32[]{:S(2)}) copy-start(u32[128]{0:T(128)} %constant.233) | copy-start | bytes 1540
  156.0 42.9 %all-to-all-start = ((bf16[4,450,288]{1,2,0:T(8,128)(2,1)}), bf16[4,450,288]{1,2,0:T(8,128)(2,1)S(1)}, u32[]{:S(2)}, u32[]{:S(2)}) async-start(bf16[4,450,288]{1,2,0:T(8,128)(2,1)} %broadcast_in_dim.32), calls=%async_computation | async-start | bytes 2359296 | tf_op jit(solution)/shard_map/all_to_all | solution.py:15
  238.5 21.0 %copy-start.1 = (f32[288,288]{0,1:T(8,128)}, f32[288,288]{0,1:T(8,128)S(1)}, u32[]{:S(2)}) copy-start(f32[288,288]{0,1:T(8,128)S(1)} %fusion.4) | copy-start | bytes 995332
  277.4 39.4 %copy-start = (f32[2048,288]{0,1:T(8,128)}, f32[2048,288]{0,1:T(8,128)S(1)}, u32[]{:S(2)}) copy-start(f32[2048,288]{0,1:T(8,128)S(1)} %get-tuple-element.86) | copy-start | bytes 7077892
Sparse Core Ops, SparseCore 0:
  28.0 63.2 all-reduce.9
  93.6 40.5 all-reduce.11
  140.8 51.7 reduce-scatter.3
  194.8 37.9 reduce-scatter.5
  235.1 38.0 reduce-scatter.7
